TPU v7x, 32 devices: a whole 2x2x4 slice. The times are simulated.
32 devices in a mesh: fsdp: 16 (over z, y, x), rep: 2 (over core).
Axes of the slice: x: 2, y: 2, z: 4, core: 2. Of those that a mesh axis runs over, the one named last changes fastest.
Arguments:
- params: float32 [1536, 3584], P(('fsdp', 'rep')), may hold values from -6 to 6
- grads: bfloat16 [1536, 3584], P(('fsdp', 'rep')), may hold values from -6 to 6
- moments: bfloat16 [3, 1536, 3584], P(None, ('fsdp', 'rep')), may hold values from -6 to 6
- row_acc: float32 [1536], P(('fsdp', 'rep')), may hold values from 0.05 to 1
- lengths: int32 [32], replicated, may hold values from 1 to 384, 1536 in all
- tensor_order: int32 [32], replicated, may hold values from 0 to 31, each once
- col_acc: float32 [32, 3584], P('fsdp'), may hold values from 0.05 to 1
- hidden_state: float32 [32, 512], P('fsdp'), may hold values from -1 to 1
- cell_state: float32 [32, 512], P('fsdp'), may hold values from -4 to 4
- lstm_in: bfloat16 [10, 2048], replicated, may hold values from -2 to 2
- lstm_rec: bfloat16 [512, 2048], replicated, may hold values from -0.25 to 0.25
- lstm_bias: float32 [2048], replicated, may hold values from -3 to 3
- hyper_first: bfloat16 [512, 256], replicated, may hold values from -0.25 to 0.25
- hyper_rest: bfloat16 [512, 128], replicated, may hold values from -0.25 to 0.25
Outputs:
- update: float32 [1536, 3584], P(('fsdp', 'rep'))
- row_new: float32 [1536], P(('fsdp', 'rep'))
- col_new: float32 [32, 3584], P('fsdp')
- hidden_new: float32 [32, 512], P('fsdp')
- cell_new: float32 [32, 512], P('fsdp')
Inputs may be any that keep to these rules, and one draw needn't show every extreme that they name: `lengths`: they sum to 1536; the largest is 384. `tensor_order`: owner slot i belongs to fsdp index i // 2; each tensor appears once.
All inputs are finite; a program needn't handle non-finite values.
Results may differ from a plain program's by a relative error of at most 0.019.
Values may be sent and summed in bfloat16 or wider, within the bound.
A program may use at most 64 MiB of HBM per device.

v0:
```python
import math
import jax
import jax.numpy as jnp
from jax import lax
from jax.sharding import PartitionSpec as P

EPSILON = 1e-06
DECAY_RATE = 0.9


def owner_step(
    col_sums,
    tensor_stats,
    row_lengths,
    col_acc,
    hidden_state,
    cell_state,
    lstm_in,
    lstm_rec,
    lstm_bias,
    hyper_first,
    hyper_rest,
):
    col_width = col_acc.shape[1]
    col_new = DECAY_RATE * col_acc + (1.0 - DECAY_RATE) * col_sums / row_lengths[:, None]
    tensor_means = tensor_stats / (row_lengths * col_width)[:, None]
    log_means = jnp.log(tensor_means[:, :5] + EPSILON)
    corr_first = tensor_means[:, 5] / jnp.sqrt(tensor_means[:, 0] * tensor_means[:, 1] + EPSILON)
    corr_second = tensor_means[:, 6] / jnp.sqrt(tensor_means[:, 0] * tensor_means[:, 3] + EPSILON)
    corr_third = tensor_means[:, 7] / jnp.sqrt(tensor_means[:, 1] * tensor_means[:, 3] + EPSILON)
    col_mean = jnp.mean(col_new, axis=1)
    col_square = jnp.mean(col_new * col_new, axis=1)
    spread = jnp.log(col_square / (col_mean * col_mean))
    extra = jnp.stack(
        [corr_first, corr_second, corr_third, jnp.log(col_mean + EPSILON), spread], axis=1
    )
    features = jnp.concatenate([log_means, extra], axis=1).astype(jnp.bfloat16)
    gate_sum = jnp.dot(features, lstm_in, preferred_element_type=jnp.float32)
    gate_sum = (
        gate_sum
        + jnp.dot(hidden_state.astype(jnp.bfloat16), lstm_rec, preferred_element_type=jnp.float32)
        + lstm_bias
    )
    hid_width = hidden_state.shape[1]
    gate_in = gate_sum[:, :hid_width]
    gate_forget = gate_sum[:, hid_width : 2 * hid_width]
    gate_cand = gate_sum[:, 2 * hid_width : 3 * hid_width]
    gate_out = gate_sum[:, 3 * hid_width :]
    cell_new = jax.nn.sigmoid(gate_forget) * cell_state + jax.nn.sigmoid(gate_in) * jnp.tanh(
        gate_cand
    )
    hidden_new = jax.nn.sigmoid(gate_out) * jnp.tanh(cell_new)
    hidden_bf = hidden_new.astype(jnp.bfloat16)
    gen_first = jnp.dot(hidden_bf, hyper_first, preferred_element_type=jnp.float32).astype(
        jnp.bfloat16
    )
    gen_rest = jnp.dot(hidden_bf, hyper_rest, preferred_element_type=jnp.float32).astype(
        jnp.bfloat16
    )
    tensor_scales = jnp.stack(
        [
            jnp.sqrt(tensor_means[:, 0] + EPSILON),
            jnp.sqrt(tensor_means[:, 1] + EPSILON),
            jnp.sqrt(tensor_means[:, 4] + EPSILON),
            col_mean,
        ],
        axis=1,
    )
    return (col_new, hidden_new, cell_new, gen_first, gen_rest, tensor_scales)


def param_block(
    param_rows, grad_rows, moment_rows, row_var, col_rows, first_rows, rest_rows, scale_rows
):
    block_rows = param_rows.shape[0]
    grad_f = grad_rows.astype(jnp.float32)
    mom_f = moment_rows.astype(jnp.float32)
    v_factored = row_var[:, None] * col_rows / scale_rows[:, 3:4]
    inv_rms = lax.rsqrt(v_factored + EPSILON)
    grad_norm = grad_f * inv_rms
    mom_norm = mom_f[0] * inv_rms
    inputs = jnp.stack(
        [
            grad_norm,
            mom_norm,
            mom_f[1] * inv_rms,
            mom_f[2] * inv_rms,
            grad_f / scale_rows[:, 0:1],
            mom_f[0] / scale_rows[:, 1:2],
            param_rows / scale_rows[:, 2:3],
            grad_norm * mom_norm,
        ],
        axis=1,
    ).astype(jnp.bfloat16)
    hm_width = rest_rows.shape[1] // 4
    w_first = first_rows.reshape(block_rows, 8, hm_width)
    bias_first = rest_rows[:, :hm_width].astype(jnp.float32)
    w_second = rest_rows[:, hm_width:].reshape(block_rows, hm_width, 3)
    hidden_units = (
        jnp.einsum("bfc,bfh->bhc", inputs, w_first, preferred_element_type=jnp.float32)
        + bias_first[:, :, None]
    )
    hidden_units = jax.nn.relu(hidden_units).astype(jnp.bfloat16)
    mlp_out = jnp.einsum("bhc,bho->boc", hidden_units, w_second, preferred_element_type=jnp.float32)
    return mlp_out[:, 0] * jnp.exp(jnp.tanh(mlp_out[:, 1])) * jax.nn.sigmoid(mlp_out[:, 2])


def on_device(
    params,
    grads,
    moments,
    row_acc,
    lengths,
    tensor_order,
    col_acc,
    hidden_state,
    cell_state,
    lstm_in,
    lstm_rec,
    lstm_bias,
    hyper_first,
    hyper_rest,
):
    row_count = params.shape[0]
    tensor_count = lengths.shape[0]
    own_count = col_acc.shape[0]
    first_row = (lax.axis_index("fsdp") * lax.axis_size("rep") + lax.axis_index("rep")) * row_count
    tensor_ends = jnp.cumsum(lengths)
    global_rows = first_row + lax.iota(jnp.int32, row_count)
    seg_ids = jnp.sum((global_rows[:, None] >= tensor_ends[None, :]).astype(jnp.int32), axis=1)
    row_pick = (seg_ids[:, None] == tensor_order[None, :]).astype(jnp.float32)
    slot_match = tensor_order[:, None] == lax.iota(jnp.int32, tensor_count)[None, :]
    row_lengths = jnp.sum(jnp.where(slot_match, lengths[None, :], 0), axis=1).astype(jnp.float32)
    grad_f = grads.astype(jnp.float32)
    grad_sq = grad_f * grad_f
    row_new = DECAY_RATE * row_acc + (1.0 - DECAY_RATE) * jnp.mean(grad_sq, axis=1)
    mom_zero = moments[0].astype(jnp.float32)
    mom_one = moments[1].astype(jnp.float32)
    mom_two = moments[2].astype(jnp.float32)
    per_row = jnp.stack(
        [
            jnp.sum(grad_sq, axis=1),
            jnp.sum(mom_zero * mom_zero, axis=1),
            jnp.sum(mom_one * mom_one, axis=1),
            jnp.sum(mom_two * mom_two, axis=1),
            jnp.sum(params * params, axis=1),
            jnp.sum(grad_f * mom_zero, axis=1),
            jnp.sum(grad_f * mom_two, axis=1),
            jnp.sum(mom_zero * mom_two, axis=1),
        ],
        axis=1,
    )
    slot_stats = jnp.einsum("ri,rk->ik", row_pick, per_row, precision=lax.Precision.HIGHEST)
    slot_cols = jnp.einsum("ri,rc->ic", row_pick, grad_sq, precision=lax.Precision.HIGHEST)
    mine_start = lax.axis_index("fsdp") * own_count
    col_total, stats_total = lax.psum((slot_cols, slot_stats), ("fsdp", "rep"))
    col_prev, hidden_all, cell_all = (
        lax.all_gather(col_acc, "fsdp", axis=0, tiled=True),
        lax.all_gather(hidden_state, "fsdp", axis=0, tiled=True),
        lax.all_gather(cell_state, "fsdp", axis=0, tiled=True),
    )
    col_all, hidden_every, cell_every, first_all, rest_all, scale_all = owner_step(
        col_total,
        stats_total,
        row_lengths,
        col_prev,
        hidden_all,
        cell_all,
        lstm_in,
        lstm_rec,
        lstm_bias,
        hyper_first,
        hyper_rest,
    )
    col_new = lax.dynamic_slice_in_dim(col_all, mine_start, own_count, 0)
    hidden_new = lax.dynamic_slice_in_dim(hidden_every, mine_start, own_count, 0)
    cell_new = lax.dynamic_slice_in_dim(cell_every, mine_start, own_count, 0)
    col_rows = jnp.dot(row_pick, col_all, precision=lax.Precision.HIGHEST)
    scale_rows = jnp.dot(row_pick, scale_all, precision=lax.Precision.HIGHEST)
    pick_bf = row_pick.astype(jnp.bfloat16)
    first_rows = jnp.dot(pick_bf, first_all, preferred_element_type=jnp.float32).astype(
        jnp.bfloat16
    )
    rest_rows = jnp.dot(pick_bf, rest_all, preferred_element_type=jnp.float32).astype(jnp.bfloat16)
    block_rows = math.gcd(row_count, 16)
    block_count = row_count // block_rows

    def one_block(index):
        start = index * block_rows
        return param_block(
            lax.dynamic_slice_in_dim(params, start, block_rows, 0),
            lax.dynamic_slice_in_dim(grads, start, block_rows, 0),
            lax.dynamic_slice_in_dim(moments, start, block_rows, 1),
            lax.dynamic_slice_in_dim(row_new, start, block_rows, 0),
            lax.dynamic_slice_in_dim(col_rows, start, block_rows, 0),
            lax.dynamic_slice_in_dim(first_rows, start, block_rows, 0),
            lax.dynamic_slice_in_dim(rest_rows, start, block_rows, 0),
            lax.dynamic_slice_in_dim(scale_rows, start, block_rows, 0),
        )

    update = lax.map(one_block, lax.iota(jnp.int32, block_count)).reshape(params.shape)
    return (update, row_new, col_new, hidden_new, cell_new)


def solution(mesh):
    placed = (
        P(("fsdp", "rep"), None),
        P(("fsdp", "rep"), None),
        P(None, ("fsdp", "rep"), None),
        P(("fsdp", "rep")),
        P(),
        P(),
        P("fsdp", None),
        P("fsdp", None),
        P("fsdp", None),
        P(),
        P(),
        P(),
        P(),
        P(),
    )
    return jax.shard_map(
        on_device,
        mesh=mesh,
        in_specs=placed,
        out_specs=(
            P(("fsdp", "rep"), None),
            P(("fsdp", "rep")),
            P("fsdp", None),
            P("fsdp", None),
            P("fsdp", None),
        ),
        check_vma=False,
    )
```

profile of v0, /device:TPU:0, one launch (start us, length us, event | category | flops | bytes accessed | tf_op | source)
XLA Modules:
  0.0 245.1 jit_solution(586881530292995540)
XLA Ops:
  7.3 0.9 copy.76
  8.4 2.3 fusion.25
  10.7 0.9 select_reduce_fusion
  11.6 1.2 multiply_reduce_fusion.1
  12.7 1.7 fusion.30
  14.4 1.2 multiply_reduce_fusion
  16.5 42.0 %psum.14 = f32[32,8]{0,1:T(8,128)S(1)} all-reduce(f32[32,8]{0,1:T(8,128)S(1)} %fusion.50), channel_id=1, replica_groups=mesh['fsdp'=16,'rep'=2] {'fsdp','rep'}, use_global_device_ids=true, to_apply=%region_12.13 | all-reduce | flops 256 | bytes 2048 | tf_op jit(solution)/shard_map/psum | solution.py:156
  59.1 39.8 %all-gather.1 = bf16[16,2,512]{2,1,0:T(2,128)(2,1)S(1)} all-gather(bf16[1,2,512]{2,1,0:T(2,128)(2,1)S(1)} %bitcast_convert_fusion), channel_id=1, replica_groups=mesh['fsdp'=16,'rep'=2] {'fsdp'}, dimensions={0}, use_global_device_ids=true | all-gather | bytes 34816 | tf_op jit(solution)/shard_map/all_gather | solution.py:159
  98.9 38.4 %all-gather = f32[16,2,3584]{2,1,0:T(2,128)S(1)} all-gather(f32[1,2,3584]{2,1,0:T(2,128)S(1)} %bitcast.121), channel_id=1, replica_groups=mesh['fsdp'=16,'rep'=2] {'fsdp'}, dimensions={0}, use_global_device_ids=true | all-gather | bytes 487424 | tf_op jit(solution)/shard_map/all_gather | solution.py:158
  138.1 37.8 %all-gather.2 = f32[16,2,512]{2,1,0:T(2,128)S(1)} all-gather(f32[1,2,512]{2,1,0:T(2,128)S(1)} %bitcast.122), channel_id=1, replica_groups=mesh['fsdp'=16,'rep'=2] {'fsdp'}, dimensions={0}, use_global_device_ids=true | all-gather | bytes 69632 | tf_op jit(solution)/shard_map/all_gather | solution.py:160
  176.9 1.3 multiply_reduce_fusion.2
  178.2 2.0 fusion.47
  182.7 0.9 convolution_convert_fusion
  183.8 54.4 %while.10 = (s32[]{:T(128)}, f32[3,16,3584]{2,1,0:T(8,128)}, s32[3]{0:T(128)S(1)}, bf16[48,128]{1,0:T(8,128)(2,1)S(1)}, bf16[48,256]{1,0:T(8,128)(2,1)}, /*index...) while((s32[]{:T(128)}, f32[3,16,3584]{2,1,0:T(8,128)}, ...), condition=%wide.region_16.17_spmd, body=%wide.region_15.16_spmd.sunk | while | flops 47481352 | bytes 11314883 | solution.py:201
  187.0 1.0 dynamic-slice_convert_fusion.4
  188.4 1.3 fusion.104
  190.6 0.9 copy.132
  191.5 0.9 copy.133
  192.4 5.5 %stack.83 = bf16[16,8,3584]{2,1,0:T(8,128)(2,1)} concatenate(bf16[16,1,3584]{2,1,0:T(2,128)(2,1)S(1)} %copy.127, bf16[16,1,3584]{2,1,0:T(2,128)(2,1)S(1)} %copy.128, bf16[16,1,3584]{2,1,0:T(2,128)(2,1)S(1)} %copy.129, bf16[16,1,3584]{2,1,0:T(2,128)(2,1)S(1)} %copy.130, bf16[16,1,3584]{2,1,0:T(2,128)(2,1)S(1)} %copy.131, bf16[16,1,3584]{2,1,0:T(2,128)(2,1)S(1)} %fusion.105, ...), dimensions={1} | concatenate | bytes 1835008 | tf_op jit(solution)/shard_map/while/body/eval_jaxpr/stack | solution.py:82
  197.9 2.8 %fusion.106 = f32[16,3,3584]{2,1,0:T(4,128)S(1)} fusion(bf16[16,32,3]{1,2,0:T(4,128)(2,1)S(1)} %copy.126, bf16[16,8,32]{2,1,0:T(8,128)(2,1)S(1)} %reshape.216, bf16[16,8,3584]{2,1,0:T(8,128)(2,1)} %stack.83, f32[16,32]{1,0:T(8,128)S(1)} %dynamic-slice_convert_fusion.5), kind=kOutput, calls=%fused_computation.1.clone.1 | convolution fusion | flops 45875200 | bytes 1618944 | tf_op jit(solution)/shard_map/while/body/eval_jaxpr/bhc,bho->boc/dot_general | solution.py:104
  205.2 1.0 dynamic-slice_convert_fusion.4
  206.5 1.3 fusion.104
  208.8 0.9 copy.132
  209.7 0.9 copy.133
  210.5 5.5 %stack.83 = bf16[16,8,3584]{2,1,0:T(8,128)(2,1)} concatenate(bf16[16,1,3584]{2,1,0:T(2,128)(2,1)S(1)} %copy.127, bf16[16,1,3584]{2,1,0:T(2,128)(2,1)S(1)} %copy.128, bf16[16,1,3584]{2,1,0:T(2,128)(2,1)S(1)} %copy.129, bf16[16,1,3584]{2,1,0:T(2,128)(2,1)S(1)} %copy.130, bf16[16,1,3584]{2,1,0:T(2,128)(2,1)S(1)} %copy.131, bf16[16,1,3584]{2,1,0:T(2,128)(2,1)S(1)} %fusion.105, ...), dimensions={1} | concatenate | bytes 1835008 | tf_op jit(solution)/shard_map/while/body/eval_jaxpr/stack | solution.py:82
  216.0 2.8 %fusion.106 = f32[16,3,3584]{2,1,0:T(4,128)S(1)} fusion(bf16[16,32,3]{1,2,0:T(4,128)(2,1)S(1)} %copy.126, bf16[16,8,32]{2,1,0:T(8,128)(2,1)S(1)} %reshape.216, bf16[16,8,3584]{2,1,0:T(8,128)(2,1)} %stack.83, f32[16,32]{1,0:T(8,128)S(1)} %dynamic-slice_convert_fusion.5), kind=kOutput, calls=%fused_computation.1.clone.1 | convolution fusion | flops 45875200 | bytes 1618944 | tf_op jit(solution)/shard_map/while/body/eval_jaxpr/bhc,bho->boc/dot_general | solution.py:104
  223.3 1.0 dynamic-slice_convert_fusion.4
  224.7 1.3 fusion.104
  226.9 0.9 copy.132
  227.8 0.9 copy.133
  228.7 5.5 %stack.83 = bf16[16,8,3584]{2,1,0:T(8,128)(2,1)} concatenate(bf16[16,1,3584]{2,1,0:T(2,128)(2,1)S(1)} %copy.127, bf16[16,1,3584]{2,1,0:T(2,128)(2,1)S(1)} %copy.128, bf16[16,1,3584]{2,1,0:T(2,128)(2,1)S(1)} %copy.129, bf16[16,1,3584]{2,1,0:T(2,128)(2,1)S(1)} %copy.130, bf16[16,1,3584]{2,1,0:T(2,128)(2,1)S(1)} %copy.131, bf16[16,1,3584]{2,1,0:T(2,128)(2,1)S(1)} %fusion.105, ...), dimensions={1} | concatenate | bytes 1835008 | tf_op jit(solution)/shard_map/while/body/eval_jaxpr/stack | solution.py:82
  234.2 2.8 %fusion.106 = f32[16,3,3584]{2,1,0:T(4,128)S(1)} fusion(bf16[16,32,3]{1,2,0:T(4,128)(2,1)S(1)} %copy.126, bf16[16,8,32]{2,1,0:T(8,128)(2,1)S(1)} %reshape.216, bf16[16,8,3584]{2,1,0:T(8,128)(2,1)} %stack.83, f32[16,32]{1,0:T(8,128)S(1)} %dynamic-slice_convert_fusion.5), kind=kOutput, calls=%fused_computation.1.clone.1 | convolution fusion | flops 45875200 | bytes 1618944 | tf_op jit(solution)/shard_map/while/body/eval_jaxpr/bhc,bho->boc/dot_general | solution.py:104
  (116 shorter events, 21.2 us)
Async XLA Ops:
  7.2 130.4 %copy-start = (bf16[512,2048]{1,0:T(8,128)(2,1)S(1)}, bf16[512,2048]{1,0:T(8,128)(2,1)}, u32[]{:S(2)}) copy-start(bf16[512,2048]{1,0:T(8,128)(2,1)} %param.26) | copy-start | bytes 6291460
  7.2 9.1 %copy-start.6 = (s32[32]{0:T(128)S(1)}, s32[32]{0:T(128)}, u32[]{:S(2)}) copy-start(s32[32]{0:T(128)} %param.21) | copy-start | bytes 388
  7.2 8.5 %copy-start.10 = (f32[2,512]{1,0:T(2,128)S(1)}, f32[2,512]{1,0:T(2,128)}, u32[]{:S(2)}) copy-start(f32[2,512]{1,0:T(2,128)} %param.23) | copy-start | bytes 12292
  7.2 8.5 %copy-start.11 = (f32[48]{0:T(128)S(1)}, f32[48]{0:T(128)}, u32[]{:S(2)}) copy-start(f32[48]{0:T(128)} %param.19) | copy-start | bytes 580
  7.2 91.7 %copy-start.4 = (f32[2,3584]{1,0:T(2,128)S(1)}, f32[2,3584]{1,0:T(2,128)}, u32[]{:S(2)}) copy-start(f32[2,3584]{1,0:T(2,128)} %param.22) | copy-start | bytes 86020
  7.2 169.6 %all-reduce.2.cloned.1.call-start = ((), (), s32[]{:S(2)}) async-start(), calls=%async_computation | async-start | bytes 917504 | tf_op jit(solution)/shard_map/psum | solution.py:156
  8.4 7.9 %copy-start.7 = (s32[48]{0:T(128)}, s32[48]{0:T(128)S(1)}, u32[]{:S(2)}) copy-start(s32[48]{0:T(128)S(1)} %convert_reduce_fusion) | copy-start | bytes 580
  15.7 122.4 %copy-start.9 = (f32[2,512]{1,0:T(2,128)S(1)}, f32[2,512]{1,0:T(2,128)}, u32[]{:S(2)}) copy-start(f32[2,512]{1,0:T(2,128)} %param.24) | copy-start | bytes 12292
  138.0 43.5 %copy-start.3 = (bf16[10,2048]{1,0:T(8,128)(2,1)S(1)}, bf16[10,2048]{1,0:T(8,128)(2,1)}, u32[]{:S(2)}) copy-start(bf16[10,2048]{1,0:T(8,128)(2,1)} %param.25) | copy-start | bytes 122884
  138.0 43.5 %copy-start.5 = (f32[2048]{0:T(1024)S(1)}, f32[2048]{0:T(1024)}, u32[]{:S(2)}) copy-start(f32[2048]{0:T(1024)} %param.27) | copy-start | bytes 24580
  176.5 6.0 %copy-start.2 = (bf16[512,128]{1,0:T(8,128)(2,1)S(1)}, bf16[512,128]{1,0:T(8,128)(2,1)}, u32[]{:S(2)}) copy-start(bf16[512,128]{1,0:T(8,128)(2,1)} %param.29) | copy-start | bytes 393220
  176.8 5.7 %copy-start.8 = (s32[48]{0:T(128)S(1)}, s32[48]{0:T(128)}, u32[]{:S(2)}) copy-start(s32[48]{0:T(128)} %copy-done.7) | copy-start | bytes 580
  176.8 5.9 %copy-start.1 = (bf16[512,256]{1,0:T(8,128)(2,1)S(1)}, bf16[512,256]{1,0:T(8,128)(2,1)}, u32[]{:S(2)}) copy-start(bf16[512,256]{1,0:T(8,128)(2,1)} %param.28) | copy-start | bytes 786436
Sparse Core Ops, SparseCore 0:
  13.3 130.1 all-reduce.1
where the time goes:
time: 247 us; the launch traced here: 245 us
  blocking collectives  158 us (64%)
  local copies, waits for them, and re-layouts  36.7 us (15%)
  other arithmetic  19 us (8%)
  matrix products  14.8 us (6%)
  between operations  14.3 us (6%)
    psum x1, blocking collectives, on_device(): col_total, stats_total = lax.psum((slot_cols, slot_stats), ('fsdp', 'rep'))  42 us
    all_gather x1, blocking collectives, on_device(): lax.all_gather(hidden_state, 'fsdp', axis=0, tiled=True)  39.8 us
    all_gather x1, blocking collectives, on_device(): lax.all_gather(col_acc, 'fsdp', axis=0, tiled=True)  38.4 us
    all_gather x1, blocking collectives, on_device(): lax.all_gather(cell_state, 'fsdp', axis=0, tiled=True)  37.8 us
    another operation x24, local copies, waits for them, and re-layouts, param_block(): jnp.stack([grad_norm, mom_norm, mom_f[1] * inv_rms, mom_f[2] * inv_rms, g...  24.4 us
    dot_general x3, matrix products, param_block(): jnp.einsum('bhc,bho->boc', hidden_units, w_second, preferred_element_type...  8.4 us
  transfers between devices with their start and end apart: 1, of which 0 were waited for; matrix products, arithmetic and copies ran while one was open for 3% of the time, Pallas kernels for 0%

commit v1 on v0

--- a/solution.py
+++ b/solution.py
@@ -153,7 +153,7 @@
     slot_stats = jnp.einsum("ri,rk->ik", row_pick, per_row, precision=lax.Precision.HIGHEST)
     slot_cols = jnp.einsum("ri,rc->ic", row_pick, grad_sq, precision=lax.Precision.HIGHEST)
     mine_start = lax.axis_index("fsdp") * own_count
-    col_total, stats_total = lax.psum((slot_cols, slot_stats), ("fsdp", "rep"))
+    col_total, stats_total = lax.psum(lax.psum((slot_cols, slot_stats), "fsdp"), "rep")
     col_prev, hidden_all, cell_all = (
         lax.all_gather(col_acc, "fsdp", axis=0, tiled=True),
         lax.all_gather(hidden_state, "fsdp", axis=0, tiled=True),

time: 247 us -> 256 us (1.036)
  waiting for transfers between devices: 0.04 us -> 15.9 us
  local copies, waits for them, and re-layouts: 36.7 us -> 32.5 us
    psum x1 -> x2, waiting for transfers between devices: 0.02 us -> 15.9 us  [the longest x1 15.8 us: on_device(): lax.psum(lax.psum((slot_cols, slot_stats), 'fsdp'), 'rep')]
    all_gather x1, blocking collectives: 39.8 us -> 35.7 us  [on_device(): lax.all_gather(hidden_state, 'fsdp', axis=0, tiled=True)]
    psum x1 -> x2, blocking collectives: 42 us -> 46 us  [the longest x1 43.5 us: on_device(): lax.psum((slot_cols, slot_stats), 'fsdp')]
  transfers between devices with their start and end apart: 1 -> 2, of which waited for: 0 -> 1; matrix products, arithmetic and copies ran while one was open for 3% -> 2% of each run, Pallas kernels for 0% -> 0%
where the time goes in v1:
time: 256 us; the launch traced here: 254 us
  blocking collectives  158 us (62%)
  local copies, waits for them, and re-layouts  32.5 us (13%)
  other arithmetic  17.3 us (7%)
  waiting for transfers between devices  15.9 us (6%)
  between operations  14.3 us (6%)
  matrix products  13.6 us (5%)
    psum x1, blocking collectives, on_device(): lax.psum((slot_cols, slot_stats), 'fsdp')  43.5 us
    all_gather x1, blocking collectives, on_device(): lax.all_gather(col_acc, 'fsdp', axis=0, tiled=True)  40.7 us
    all_gather x1, blocking collectives, on_device(): lax.all_gather(cell_state, 'fsdp', axis=0, tiled=True)  35.8 us
    all_gather x1, blocking collectives, on_device(): lax.all_gather(hidden_state, 'fsdp', axis=0, tiled=True)  35.7 us
    another operation x24, local copies, waits for them, and re-layouts, param_block(): jnp.stack([grad_norm, mom_norm, mom_f[1] * inv_rms, mom_f[2] * inv_rms, g...  24.4 us
    psum x1, waiting for transfers between devices, on_device(): lax.psum(lax.psum((slot_cols, slot_stats), 'fsdp'), 'rep')  15.8 us
    dot_general x3, matrix products, param_block(): jnp.einsum('bhc,bho->boc', hidden_units, w_second, preferred_element_type...  8.42 us
  transfers between devices with their start and end apart: 2, of which 1 were waited for; matrix products, arithmetic and copies ran while one was open for 2% of the time, Pallas kernels for 0%

profile of v1, /device:TPU:0, one launch (start us, length us, event | category | flops | bytes accessed | tf_op | source)
XLA Modules:
  0.0 254.1 jit_solution(17385882150223232363)
XLA Ops:
  7.3 0.9 copy.76
  8.4 2.3 fusion.25
  11.6 1.2 multiply_reduce_fusion.1
  12.8 1.7 fusion.30
  14.5 1.2 multiply_reduce_fusion
  16.0 43.5 %psum.28 = f32[32,8]{0,1:T(8,128)S(1)} all-reduce(f32[32,8]{0,1:T(8,128)S(1)} %fusion.50), channel_id=1, replica_groups=mesh['fsdp'=16,'rep'=2] {'fsdp'}, use_global_device_ids=true, to_apply=%region_13.14 | all-reduce | flops 256 | bytes 2048 | tf_op jit(solution)/shard_map/psum | solution.py:156
  59.5 2.5 psum.29
  62.0 35.8 %all-gather.2 = f32[16,2,512]{2,1,0:T(2,128)S(1)} all-gather(f32[1,2,512]{2,1,0:T(2,128)S(1)} %bitcast.122), channel_id=1, replica_groups=mesh['fsdp'=16,'rep'=2] {'fsdp'}, dimensions={0}, use_global_device_ids=true | all-gather | bytes 69632 | tf_op jit(solution)/shard_map/all_gather | solution.py:160
  97.8 40.7 %all-gather = f32[16,2,3584]{2,1,0:T(2,128)S(1)} all-gather(f32[1,2,3584]{2,1,0:T(2,128)S(1)} %bitcast.121), channel_id=1, replica_groups=mesh['fsdp'=16,'rep'=2] {'fsdp'}, dimensions={0}, use_global_device_ids=true | all-gather | bytes 487424 | tf_op jit(solution)/shard_map/all_gather | solution.py:158
  138.7 35.7 %all-gather.1 = bf16[16,2,512]{2,1,0:T(2,128)(2,1)S(1)} all-gather(bf16[1,2,512]{2,1,0:T(2,128)(2,1)S(1)} %bitcast_convert_fusion), channel_id=1, replica_groups=mesh['fsdp'=16,'rep'=2] {'fsdp'}, dimensions={0}, use_global_device_ids=true | all-gather | bytes 34816 | tf_op jit(solution)/shard_map/all_gather | solution.py:159
  175.4 15.8 %all-reduce.5.cloned.1.call-done = f32[32,3584]{1,0:T(8,128)} async-done(((f32[32,3584]{1,0:T(8,128)}), f32[32,3584]{1,0:T(8,128)}) %all-reduce.5.cloned.1.call-update) | async-done | bytes 458768 | tf_op jit(solution)/shard_map/psum | solution.py:156
  191.3 1.3 multiply_reduce_fusion.2
  192.6 1.4 fusion.47
  196.3 50.5 %while.10 = (s32[]{:T(128)}, f32[3,16,3584]{2,1,0:T(8,128)}, s32[3]{0:T(128)S(1)}, bf16[48,128]{1,0:T(8,128)(2,1)S(1)}, bf16[48,256]{1,0:T(8,128)(2,1)S(1)}, /*i...) while((s32[]{:T(128)}, f32[3,16,3584]{2,1,0:T(8,128)}, ...), condition=%wide.region_18.19_spmd, body=%wide.region_17.18_spmd.sunk | while | flops 47481352 | bytes 11511547 | solution.py:201
  198.2 1.0 dynamic-slice_convert_fusion.4
  199.5 1.3 fusion.104
  201.8 0.9 copy.132
  202.7 0.9 copy.133
  203.5 5.5 %stack.83 = bf16[16,8,3584]{2,1,0:T(8,128)(2,1)} concatenate(bf16[16,1,3584]{2,1,0:T(2,128)(2,1)S(1)} %copy.127, bf16[16,1,3584]{2,1,0:T(2,128)(2,1)S(1)} %copy.128, bf16[16,1,3584]{2,1,0:T(2,128)(2,1)S(1)} %copy.129, bf16[16,1,3584]{2,1,0:T(2,128)(2,1)S(1)} %copy.130, bf16[16,1,3584]{2,1,0:T(2,128)(2,1)S(1)} %copy.131, bf16[16,1,3584]{2,1,0:T(2,128)(2,1)S(1)} %fusion.105, ...), dimensions={1} | concatenate | bytes 1835008 | tf_op jit(solution)/shard_map/while/body/eval_jaxpr/stack | solution.py:82
  209.0 2.8 %fusion.106 = f32[16,3,3584]{2,1,0:T(4,128)S(1)} fusion(bf16[16,32,3]{1,2,0:T(4,128)(2,1)S(1)} %copy.126, bf16[16,8,32]{2,1,0:T(8,128)(2,1)S(1)} %reshape.216, bf16[16,8,3584]{2,1,0:T(8,128)(2,1)} %stack.83, f32[16,32]{1,0:T(8,128)S(1)} %dynamic-slice_convert_fusion.5), kind=kOutput, calls=%fused_computation.1.clone.1 | convolution fusion | flops 45875200 | bytes 1618944 | tf_op jit(solution)/shard_map/while/body/eval_jaxpr/bhc,bho->boc/dot_general | solution.py:104
  215.0 1.0 dynamic-slice_convert_fusion.4
  216.3 1.3 fusion.104
  218.6 0.9 copy.132
  219.5 0.9 copy.133
  220.3 5.5 %stack.83 = bf16[16,8,3584]{2,1,0:T(8,128)(2,1)} concatenate(bf16[16,1,3584]{2,1,0:T(2,128)(2,1)S(1)} %copy.127, bf16[16,1,3584]{2,1,0:T(2,128)(2,1)S(1)} %copy.128, bf16[16,1,3584]{2,1,0:T(2,128)(2,1)S(1)} %copy.129, bf16[16,1,3584]{2,1,0:T(2,128)(2,1)S(1)} %copy.130, bf16[16,1,3584]{2,1,0:T(2,128)(2,1)S(1)} %copy.131, bf16[16,1,3584]{2,1,0:T(2,128)(2,1)S(1)} %fusion.105, ...), dimensions={1} | concatenate | bytes 1835008 | tf_op jit(solution)/shard_map/while/body/eval_jaxpr/stack | solution.py:82
  225.8 2.8 %fusion.106 = f32[16,3,3584]{2,1,0:T(4,128)S(1)} fusion(bf16[16,32,3]{1,2,0:T(4,128)(2,1)S(1)} %copy.126, bf16[16,8,32]{2,1,0:T(8,128)(2,1)S(1)} %reshape.216, bf16[16,8,3584]{2,1,0:T(8,128)(2,1)} %stack.83, f32[16,32]{1,0:T(8,128)S(1)} %dynamic-slice_convert_fusion.5), kind=kOutput, calls=%fused_computation.1.clone.1 | convolution fusion | flops 45875200 | bytes 1618944 | tf_op jit(solution)/shard_map/while/body/eval_jaxpr/bhc,bho->boc/dot_general | solution.py:104
  231.8 1.0 dynamic-slice_convert_fusion.4
  233.2 1.3 fusion.104
  235.4 0.9 copy.132
  236.3 0.9 copy.133
  237.1 5.5 %stack.83 = bf16[16,8,3584]{2,1,0:T(8,128)(2,1)} concatenate(bf16[16,1,3584]{2,1,0:T(2,128)(2,1)S(1)} %copy.127, bf16[16,1,3584]{2,1,0:T(2,128)(2,1)S(1)} %copy.128, bf16[16,1,3584]{2,1,0:T(2,128)(2,1)S(1)} %copy.129, bf16[16,1,3584]{2,1,0:T(2,128)(2,1)S(1)} %copy.130, bf16[16,1,3584]{2,1,0:T(2,128)(2,1)S(1)} %copy.131, bf16[16,1,3584]{2,1,0:T(2,128)(2,1)S(1)} %fusion.105, ...), dimensions={1} | concatenate | bytes 1835008 | tf_op jit(solution)/shard_map/while/body/eval_jaxpr/stack | solution.py:82
  242.6 2.8 %fusion.106 = f32[16,3,3584]{2,1,0:T(4,128)S(1)} fusion(bf16[16,32,3]{1,2,0:T(4,128)(2,1)S(1)} %copy.126, bf16[16,8,32]{2,1,0:T(8,128)(2,1)S(1)} %reshape.216, bf16[16,8,3584]{2,1,0:T(8,128)(2,1)} %stack.83, f32[16,32]{1,0:T(8,128)S(1)} %dynamic-slice_convert_fusion.5), kind=kOutput, calls=%fused_computation.1.clone.1 | convolution fusion | flops 45875200 | bytes 1618944 | tf_op jit(solution)/shard_map/while/body/eval_jaxpr/bhc,bho->boc/dot_general | solution.py:104
  (130 shorter events, 16.6 us)
Async XLA Ops:
  7.2 167.8 %copy-start = (bf16[512,2048]{1,0:T(8,128)(2,1)S(1)}, bf16[512,2048]{1,0:T(8,128)(2,1)}, u32[]{:S(2)}) copy-start(bf16[512,2048]{1,0:T(8,128)(2,1)} %param.26) | copy-start | bytes 6291460
  7.2 8.6 %copy-start.8 = (s32[32]{0:T(128)S(1)}, s32[32]{0:T(128)}, u32[]{:S(2)}) copy-start(s32[32]{0:T(128)} %param.21) | copy-start | bytes 388
  7.2 8.6 %copy-start.10 = (f32[2,512]{1,0:T(2,128)S(1)}, f32[2,512]{1,0:T(2,128)}, u32[]{:S(2)}) copy-start(f32[2,512]{1,0:T(2,128)} %param.23) | copy-start | bytes 12292
  7.2 54.8 %copy-start.9 = (f32[2,512]{1,0:T(2,128)S(1)}, f32[2,512]{1,0:T(2,128)}, u32[]{:S(2)}) copy-start(f32[2,512]{1,0:T(2,128)} %param.24) | copy-start | bytes 12292
  7.2 90.6 %copy-start.6 = (f32[2,3584]{1,0:T(2,128)S(1)}, f32[2,3584]{1,0:T(2,128)}, u32[]{:S(2)}) copy-start(f32[2,3584]{1,0:T(2,128)} %param.22) | copy-start | bytes 86020
  7.2 167.6 %all-reduce.3.cloned.1.call-start = ((), (), s32[]{:S(2)}) async-start(), calls=%async_computation | async-start | bytes 917504 | tf_op jit(solution)/shard_map/psum | solution.py:156
  10.7 180.6 %all-reduce.5.cloned.1.call-start = ((), (), s32[]{:S(2)}) async-start(), calls=%async_computation.1 | async-start | bytes 917504 | tf_op jit(solution)/shard_map/psum | solution.py:156
  14.5 160.4 %copy-start.11 = (f32[48]{0:T(128)S(1)}, f32[48]{0:T(128)}, u32[]{:S(2)}) copy-start(f32[48]{0:T(128)} %param.19) | copy-start | bytes 580
  174.9 19.7 %copy-start.5 = (bf16[10,2048]{1,0:T(8,128)(2,1)S(1)}, bf16[10,2048]{1,0:T(8,128)(2,1)}, u32[]{:S(2)}) copy-start(bf16[10,2048]{1,0:T(8,128)(2,1)} %param.25) | copy-start | bytes 122884
  174.9 19.7 %copy-start.7 = (f32[2048]{0:T(1024)S(1)}, f32[2048]{0:T(1024)}, u32[]{:S(2)}) copy-start(f32[2048]{0:T(1024)} %param.27) | copy-start | bytes 24580
  175.4 20.1 %copy-start.4 = (bf16[512,128]{1,0:T(8,128)(2,1)S(1)}, bf16[512,128]{1,0:T(8,128)(2,1)}, u32[]{:S(2)}) copy-start(bf16[512,128]{1,0:T(8,128)(2,1)} %param.29) | copy-start | bytes 393220
  175.4 20.4 %copy-start.1 = (bf16[512,256]{1,0:T(8,128)(2,1)S(1)}, bf16[512,256]{1,0:T(8,128)(2,1)}, u32[]{:S(2)}) copy-start(bf16[512,256]{1,0:T(8,128)(2,1)} %param.28) | copy-start | bytes 786436
  196.3 4.6 %copy-start.2 = (bf16[48,256]{1,0:T(8,128)(2,1)}, bf16[48,256]{1,0:T(8,128)(2,1)S(1)}, u32[]{:S(2)}) copy-start(bf16[48,256]{1,0:T(8,128)(2,1)S(1)} %get-tuple-element.295) | copy-start | bytes 73732 | tf_op jit(solution)/shard_map/while
  209.0 4.1 %copy-start.3 = (bf16[48,256]{1,0:T(8,128)(2,1)S(1)}, bf16[48,256]{1,0:T(8,128)(2,1)}, u32[]{:S(2)}) copy-start(bf16[48,256]{1,0:T(8,128)(2,1)} %copy-done.2) | copy-start | bytes 73732 | tf_op jit(solution)/shard_map/while
  213.1 4.5 %copy-start.2 = (bf16[48,256]{1,0:T(8,128)(2,1)}, bf16[48,256]{1,0:T(8,128)(2,1)S(1)}, u32[]{:S(2)}) copy-start(bf16[48,256]{1,0:T(8,128)(2,1)S(1)} %get-tuple-element.295) | copy-start | bytes 73732 | tf_op jit(solution)/shard_map/while
  225.8 4.1 %copy-start.3 = (bf16[48,256]{1,0:T(8,128)(2,1)S(1)}, bf16[48,256]{1,0:T(8,128)(2,1)}, u32[]{:S(2)}) copy-start(bf16[48,256]{1,0:T(8,128)(2,1)} %copy-done.2) | copy-start | bytes 73732 | tf_op jit(solution)/shard_map/while
  229.9 4.5 %copy-start.2 = (bf16[48,256]{1,0:T(8,128)(2,1)}, bf16[48,256]{1,0:T(8,128)(2,1)S(1)}, u32[]{:S(2)}) copy-start(bf16[48,256]{1,0:T(8,128)(2,1)S(1)} %get-tuple-element.295) | copy-start | bytes 73732 | tf_op jit(solution)/shard_map/while
  242.6 4.1 %copy-start.3 = (bf16[48,256]{1,0:T(8,128)(2,1)S(1)}, bf16[48,256]{1,0:T(8,128)(2,1)}, u32[]{:S(2)}) copy-start(bf16[48,256]{1,0:T(8,128)(2,1)} %copy-done.2) | copy-start | bytes 73732 | tf_op jit(solution)/shard_map/while
  246.8 0.5 copy-start.12
Sparse Core Ops, SparseCore 0:
  13.2 111.7 all-reduce.2
  175.0 16.2 all-reduce.4
